TPU v7x, 32 devices: a whole 2x2x4 slice. The times are simulated.
32 devices in a mesh: row: 4 (over z), col: 8 (over y, x, core).
Axes of the slice: x: 2, y: 2, z: 4, core: 2. Of those that a mesh axis runs over, the one named last changes fastest.
Arguments:
- pressure: float32 [128, 256, 512], P('row', 'col'), may hold values from -6 to 6
- cut_exponent: int32 [4, 8, 2], P('row', 'col'), may hold values from 0 to 3
- group_map: int32 [4, 8, 2], P('row', 'col'), may hold values from 0 to 15
Outputs:
- coeffs: float32 [128, 256, 512], P('row', 'col')
- group_mass: float32 [16, 4], replicated
Inputs may be any that keep to these rules, and one draw needn't show every extreme that they name: `cut_exponent`: one exponent per block of 32 x 32 x 512 // 2 cells.
All inputs are finite; a program needn't handle non-finite values.
Results may differ from a plain program's by a relative error of at most 0.0001.
Values sent between devices are 32-bit elements; how exact they have to be, the bound alone decides.
A program may use at most 64 MiB of HBM per device.

v0:
```python
import jax
import jax.numpy as jnp
from jax import lax
from jax.sharding import PartitionSpec as P

GROUPS = 16


cut_levels = (0.25, 0.5, 1.0, 2.0)


def extended(value, sides, width):
    for axis, dim in sides:
        devices, length = (lax.axis_size(axis), value.shape[dim])
        up = [(i, (i + 1) % devices) for i in range(devices)]
        down = [(j, i) for i, j in up]
        last = lax.slice_in_dim(value, length - width, length, axis=dim)
        initial = lax.slice_in_dim(value, 0, width, axis=dim)
        before = lax.ppermute(last, axis, up)
        after = lax.ppermute(initial, axis, down)
        value = jnp.concatenate([before, value, after], axis=dim)
    return value


def slice_dim(values, axis_pos, offset, length):
    return lax.slice_in_dim(values, offset, offset + length, axis=axis_pos)


def parity_part(signal, axis_pos, which):
    length = signal.shape[axis_pos]
    return lax.slice_in_dim(signal, which, length, stride=2, axis=axis_pos)


def alternate(smooth, detail, axis_pos):
    merged = jnp.stack([smooth, detail], axis_pos + 1)
    shape = list(smooth.shape)
    shape[axis_pos] = 2 * shape[axis_pos]
    return merged.reshape(tuple(shape))


def predict_odd(padded, axis_pos, offset, length):
    near = slice_dim(padded, axis_pos, offset + 1, length) + slice_dim(
        padded, axis_pos, offset + 2, length
    )
    far_sum = slice_dim(padded, axis_pos, offset, length) + slice_dim(
        padded, axis_pos, offset + 3, length
    )
    return 0.5625 * near - 0.0625 * far_sum


def update_even(padded, axis_pos, offset, length):
    near = slice_dim(padded, axis_pos, offset + 1, length) + slice_dim(
        padded, axis_pos, offset + 2, length
    )
    far_sum = slice_dim(padded, axis_pos, offset, length) + slice_dim(
        padded, axis_pos, offset + 3, length
    )
    return 0.28125 * near - 0.03125 * far_sum


def cyclic_pad(values, axis_pos):
    length = values.shape[axis_pos]
    return jnp.concatenate(
        [slice_dim(values, axis_pos, length - 2, 2), values, slice_dim(values, axis_pos, 0, 2)],
        axis=axis_pos,
    )


def depth_table(size_z):
    ident = (
        jnp.arange(size_z, dtype=jnp.int32)[:, None] == jnp.arange(size_z, dtype=jnp.int32)[None, :]
    ).astype(jnp.float32)
    half = size_z // 2
    evens_half = lax.slice_in_dim(ident, 0, size_z, stride=2, axis=1)
    odds_half = lax.slice_in_dim(ident, 1, size_z, stride=2, axis=1)
    detail = odds_half - predict_odd(cyclic_pad(evens_half, 1), 1, 1, half)
    smooth = evens_half + update_even(cyclic_pad(detail, 1), 1, 0, half)
    return jnp.stack([smooth, detail], 2).reshape(size_z, size_z)


def shards(pressure, cut_exponent, group_map):
    signal = pressure
    evens_half = parity_part(signal, 0, 0)
    odds_half = parity_part(signal, 0, 1)
    half = evens_half.shape[0]
    padded = extended(evens_half, (("row", 0),), 2)
    detail = odds_half - predict_odd(padded, 0, 1, half)
    padded_detail = extended(detail, (("row", 0),), 2)
    smooth = evens_half + update_even(padded_detail, 0, 0, half)
    signal = alternate(smooth, detail, 0)
    evens_half = parity_part(signal, 1, 0)
    odds_half = parity_part(signal, 1, 1)
    half = evens_half.shape[1]
    padded = extended(evens_half, (("col", 1),), 2)
    detail = odds_half - predict_odd(padded, 1, 1, half)
    padded_detail = extended(detail, (("col", 1),), 2)
    smooth = evens_half + update_even(padded_detail, 1, 0, half)
    signal = alternate(smooth, detail, 1)
    size_x, size_y, size_z = signal.shape
    table = depth_table(size_z)
    coeffs = jnp.dot(
        signal.reshape(size_x * size_y, size_z),
        table,
        precision=lax.Precision.HIGHEST,
        preferred_element_type=jnp.float32,
    ).reshape(size_x, size_y, size_z)
    blocks_z = cut_exponent.shape[2]
    parity_x = (jnp.arange(size_x, dtype=jnp.int32) % 2)[:, None, None]
    parity_y = (jnp.arange(size_y, dtype=jnp.int32) % 2)[None, :, None]
    parity_z = (jnp.arange(size_z, dtype=jnp.int32) % 2)[None, None, :]
    detail_mask = parity_x + parity_y + parity_z > 0
    magnitude = jnp.where(detail_mask, jnp.abs(coeffs), jnp.float32(0.0))
    shaped = magnitude.reshape(size_x, size_y, blocks_z, size_z // blocks_z)
    scales = jnp.exp2(-cut_exponent[0, 0].astype(jnp.float32))
    cells = size_x * size_y * (size_z // blocks_z)
    block_list = []
    for level_value in cut_levels:
        limit = (level_value * scales)[None, None, :, None]
        block_list.append(jnp.sum(jnp.maximum(shaped - limit, 0.0), axis=(0, 1, 3)) / cells)
    block_mass = jnp.stack(block_list, -1)
    onehot = (group_map[0, 0][:, None] == jnp.arange(GROUPS, dtype=jnp.int32)[None, :]).astype(
        jnp.float32
    )
    partial_mass = jnp.einsum("zg,zk->gk", onehot, block_mass, precision=lax.Precision.HIGHEST)
    group_mass = lax.psum(partial_mass, ("row", "col"))
    return (coeffs, group_mass)


def solution(mesh):
    in_specs = (P("row", "col", None), P("row", "col", None), P("row", "col", None))
    out_specs = (P("row", "col", None), P())
    return jax.shard_map(shards, mesh=mesh, in_specs=in_specs, out_specs=out_specs, check_vma=False)
```

profile of v0, /device:TPU:0, one launch (start us, length us, event | category | flops | bytes accessed | tf_op | source)
XLA Modules:
  0.0 132.1 jit_solution(17617077688125911928)
XLA Ops:
  0.6 1.3 slice.136
  2.0 3.1 %collective-permute-start.1 = (f32[2,32,512]{2,1,0:T(8,128)S(1)}, f32[2,32,512]{2,1,0:T(8,128)S(1)}, u32[]{:S(2)}, u32[]{:S(2)}) collective-permute-start(f32[2,32,512]{2,1,0:T(8,128)S(1)} %get-tuple-element.14), channel_id=1, source_target_pairs={{0,8},{8,16},{16,24},{24,0},{1,9},{9,17},{17,25},{25,1},{2,10},{10... | collective-permute-start | bytes 393224 | tf_op jit(solution)/shard_map/ppermute | solution.py:19
  5.1 2.1 %collective-permute-start = (f32[2,32,512]{2,1,0:T(8,128)S(1)}, f32[2,32,512]{2,1,0:T(8,128)}, u32[]{:S(2)}, u32[]{:S(2)}) collective-permute-start(f32[2,32,512]{2,1,0:T(8,128)S(1)} %get-tuple-element.15), channel_id=1, source_target_pairs={{8,0},{16,8},{24,16},{0,24},{9,1},{17,9},{25,17},{1,25},{10,2},{18... | collective-permute-start | bytes 393224 | tf_op jit(solution)/shard_map/ppermute | solution.py:20
  7.2 0.5 and_select_fusion
  7.8 19.5 %slice.160 = f32[512,256]{1,0:T(8,128)S(1)} slice(f32[512,512]{1,0:T(8,128)S(1)} %fusion.32), slice={[0:512:1], [0:512:2]} | slice | bytes 1048576 | tf_op jit(solution)/shard_map/slice | solution.py:74
  27.3 19.5 %slice.161 = f32[512,256]{1,0:T(8,128)S(1)} slice(f32[512,512]{1,0:T(8,128)S(1)} %fusion.32), slice={[0:512:1], [1:512:2]} | slice | bytes 1048576 | tf_op jit(solution)/shard_map/slice | solution.py:75
  46.8 0.8 broadcast_add_fusion
  47.7 0.7 fusion.43
  48.6 1.4 %fusion.38 = f32[512,256,1]{1,0,2:T(8,128)} fusion(f32[512,256]{1,0:T(8,128)S(1)} %slice.160, f32[512,256]{1,0:T(8,128)S(1)} %fusion.43, f32[512,2]{1,0:T(8,128)S(1)} %get-tuple-element.17, f32[512,2]{1,0:T(8,128)S(1)} %get-tuple-element.16), kind=kLoop, calls=%fused_computation.68 | loop fusion | flops 1179648 | bytes 1581056 | tf_op jit(solution)/shard_map/stack | solution.py:78
  50.0 0.6 broadcast_bitcast_fusion
  50.7 1.3 fusion.10
  52.0 2.0 %collective-permute-start.3 = (f32[2,32,512]{2,1,0:T(8,128)S(1)}, f32[2,32,512]{2,1,0:T(8,128)S(1)}, u32[]{:S(2)}, u32[]{:S(2)}) collective-permute-start(f32[2,32,512]{2,1,0:T(8,128)S(1)} %get-tuple-element.12), channel_id=1, source_target_pairs={{8,0},{16,8},{24,16},{0,24},{9,1},{17,9},{25,17},{1,25},{10,2},{18... | collective-permute-start | bytes 393224 | tf_op jit(solution)/shard_map/ppermute | solution.py:20
  54.0 0.5 broadcast_multiply_fusion.1
  54.6 3.1 %collective-permute-done.3 = f32[2,32,512]{2,1,0:T(8,128)S(1)} collective-permute-done((f32[2,32,512]{2,1,0:T(8,128)S(1)}, f32[2,32,512]{2,1,0:T(8,128)S(1)}, u32[]{:S(2)}, u32[]{:S(2)}) %collective-permute-start.3) | collective-permute-done | bytes 131104 | tf_op jit(solution)/shard_map/ppermute | solution.py:20
  57.6 3.1 %collective-permute-done.2 = f32[2,32,512]{2,1,0:T(8,128)S(1)} collective-permute-done((f32[2,32,512]{2,1,0:T(8,128)S(1)}, f32[2,32,512]{2,1,0:T(8,128)S(1)}, u32[]{:S(2)}, u32[]{:S(2)}) %collective-permute-start.2) | collective-permute-done | bytes 131104 | tf_op jit(solution)/shard_map/ppermute | solution.py:19
  61.9 2.6 %collective-permute-start.4 = (f32[32,2,512]{2,1,0:T(2,128)S(1)}, f32[32,2,512]{2,1,0:T(2,128)}, u32[]{:S(2)}, u32[]{:S(2)}) collective-permute-start(f32[32,2,512]{2,1,0:T(2,128)S(1)} %get-tuple-element.11), channel_id=1, source_target_pairs={{1,0},{2,1},{3,2},{4,3},{5,4},{6,5},{7,6},{0,7},{9,8},{10,9},{11,1... | collective-permute-start | bytes 393224 | tf_op jit(solution)/shard_map/ppermute | solution.py:20
  64.6 1.3 broadcast_bitcast_fusion.2
  65.9 2.8 %slice.149 = f32[32,16,512]{2,1,0:T(8,128)} slice(f32[32,32,512]{2,1,0:T(8,128)S(1)} %bitcast.47), slice={[0:32:1], [1:32:2], [0:512:1]} | slice | bytes 2097152 | tf_op jit(solution)/shard_map/slice | solution.py:31
  68.7 2.0 %fusion.21 = f32[32,16,512]{2,1,0:T(8,128)S(1)} fusion(f32[32,16,512]{2,1,0:T(8,128)} %slice.149, f32[32,16,512]{2,1,0:T(8,128)S(1)} %slice.148, f32[32,2,512]{2,1,0:T(2,128)} %collective-permute-done.4, f32[32,2,512]{2,1,0:T(2,128)S(1)} %collective-permute-done.5), kind=kLoop, calls=%fused_computation.37 | loop fusion | flops 2359296 | bytes 3407872 | tf_op jit(solution)/shard_map/sub | solution.py:95
  70.9 1.2 collective-permute-start.7
  72.2 0.6 copy.18
  72.8 0.6 copy.17
  73.4 0.6 copy.20
  74.0 0.6 copy.19
  74.6 1.3 copy.13
  75.9 1.9 %reshape.144 = f32[512,512]{0,1:T(8,128)S(1)} reshape(f32[512,256,2]{0,2,1:T(2,128)} %copy.13) | data formatting | bytes 2097152 | tf_op jit(solution)/shard_map/reshape | solution.py:78
  77.8 0.6 add_select_fusion
  78.4 1.6 %fusion.16 = f32[32,16,1,512]{3,1,0,2:T(8,128)S(1)} fusion(f32[32,16,512]{2,1,0:T(8,128)S(1)} %slice.148, f32[32,16,512]{2,1,0:T(8,128)S(1)} %fusion.21, f32[32,2,512]{2,1,0:T(2,128)} %collective-permute-done.6, f32[32,2,512]{2,1,0:T(2,128)S(1)} %collective-permute-done.7), kind=kLoop, calls=%fused_computation.32 | loop fusion | flops 2359296 | bytes 3407872 | tf_op jit(solution)/shard_map/stack | solution.py:35
  80.2 1.7 %copy.12 = f32[32,16,2,512]{3,2,1,0:T(2,128)S(1)} copy(f32[32,16,2,512]{3,1,0,2:T(8,128)S(1)} %pad_maximum_fusion.1) | data formatting | bytes 4194304 | tf_op jit(solution)/shard_map/stack | solution.py:35
  82.0 2.5 %dot_general.8 = f32[32,32,512]{2,1,0:T(8,128)} reshape(f32[32,16,2,512]{3,2,1,0:T(2,128)S(1)} %copy.12) | data formatting | bytes 4194304 | tf_op jit(solution)/shard_map/dot_general | solution.py:101
  84.5 7.3 %maximum_reduce_fusion.3 = (f32[512]{0:T(512)S(1)}, f32[512]{0:T(512)S(1)}, f32[512]{0:T(512)S(1)}, f32[512]{0:T(512)S(1)}, f32[32,32,512]{2,1,0:T(8,128)}) fusion(f32[512]{0:T(512)S(1)} %bitcast.50, s32[512]{0:T(512)S(1)} %copy-done.12, s32[32,32]{1,0:T(8,128)S(1)} %broadcast_add_fusion, f32[512]{0:T(512)S(1)} %bitcast.49, f32[512]{0:T(512)S(1)} %bitcast.52, ...), kind=kOutput, calls=%fused_computation.5 | convolution fusion | flops 3229612032 | bytes 5265408 | tf_op jit(solution)/shard_map/dot_general | solution.py:101
  92.6 39.4 %psum.7 = f32[16,4]{0,1:T(4,128)} all-reduce(f32[16,4]{0,1:T(4,128)S(1)} %fusion.48), channel_id=1, replica_groups=mesh['row'=4,'col'=8] {'row','col'}, use_global_device_ids=true, to_apply=%region_8.9 | all-reduce | flops 64 | bytes 512 | tf_op jit(solution)/shard_map/psum | solution.py:125
  (65 shorter events, 2.9 us)
Async XLA Ops:
  2.0 44.8 %copy-start.13 = (s32[1,1,2]{2,1,0:T(1,128)S(1)}, s32[1,1,2]{2,1,0:T(1,128)}, u32[]{:S(2)}) copy-start(s32[1,1,2]{2,1,0:T(1,128)} %param.4) | copy-start | bytes 28
  2.0 48.7 %collective-permute-start.1 = (f32[2,32,512]{2,1,0:T(8,128)S(1)}, f32[2,32,512]{2,1,0:T(8,128)S(1)}, u32[]{:S(2)}, u32[]{:S(2)}) collective-permute-start(f32[2,32,512]{2,1,0:T(8,128)S(1)} %get-tuple-element.14), channel_id=1, source_target_pairs={{0,8},{8,16},{16,24},{24,0},{1,9},{9,17},{17,25},{25,1},{2,10},{10... | collective-permute-start | bytes 393224 | tf_op jit(solution)/shard_map/ppermute | solution.py:19
  5.1 45.6 %collective-permute-start = (f32[2,32,512]{2,1,0:T(8,128)S(1)}, f32[2,32,512]{2,1,0:T(8,128)}, u32[]{:S(2)}, u32[]{:S(2)}) collective-permute-start(f32[2,32,512]{2,1,0:T(8,128)S(1)} %get-tuple-element.15), channel_id=1, source_target_pairs={{8,0},{16,8},{24,16},{0,24},{9,1},{17,9},{25,17},{1,25},{10,2},{18... | collective-permute-start | bytes 393224 | tf_op jit(solution)/shard_map/ppermute | solution.py:20
  48.4 2.2 %copy-start = (f32[512,256]{1,0:T(8,128)}, f32[512,256]{1,0:T(8,128)S(1)}, u32[]{:S(2)}) copy-start(f32[512,256]{1,0:T(8,128)S(1)} %fusion.43) | copy-start | bytes 1572868
  48.4 2.2 %copy-start.2 = (f32[32,32,512]{2,1,0:T(8,128)S(1)}, f32[32,32,512]{2,1,0:T(8,128)}, u32[]{:S(2)}) copy-start(f32[32,32,512]{2,1,0:T(8,128)} %param.3) | copy-start | bytes 6291460
  52.0 5.7 %collective-permute-start.3 = (f32[2,32,512]{2,1,0:T(8,128)S(1)}, f32[2,32,512]{2,1,0:T(8,128)S(1)}, u32[]{:S(2)}, u32[]{:S(2)}) collective-permute-start(f32[2,32,512]{2,1,0:T(8,128)S(1)} %get-tuple-element.12), channel_id=1, source_target_pairs={{8,0},{16,8},{24,16},{0,24},{9,1},{17,9},{25,17},{1,25},{10,2},{18... | collective-permute-start | bytes 393224 | tf_op jit(solution)/shard_map/ppermute | solution.py:20
  54.0 6.8 %collective-permute-start.2 = (f32[2,32,512]{2,1,0:T(8,128)S(1)}, f32[2,32,512]{2,1,0:T(8,128)S(1)}, u32[]{:S(2)}, u32[]{:S(2)}) collective-permute-start(f32[2,32,512]{2,1,0:T(8,128)S(1)} %get-tuple-element.13), channel_id=1, source_target_pairs={{0,8},{8,16},{16,24},{24,0},{1,9},{9,17},{17,25},{25,1},{2,10},{10... | collective-permute-start | bytes 393224 | tf_op jit(solution)/shard_map/ppermute | solution.py:19
  61.9 6.8 %collective-permute-start.5 = (f32[32,2,512]{2,1,0:T(2,128)S(1)}, f32[32,2,512]{2,1,0:T(2,128)S(1)}, u32[]{:S(2)}, u32[]{:S(2)}) collective-permute-start(f32[32,2,512]{2,1,0:T(2,128)S(1)} %get-tuple-element.10), channel_id=1, source_target_pairs={{0,1},{1,2},{2,3},{3,4},{4,5},{5,6},{6,7},{7,0},{8,9},{9,10},{10,1... | collective-permute-start | bytes 393224 | tf_op jit(solution)/shard_map/ppermute | solution.py:19
  61.9 6.8 %collective-permute-start.4 = (f32[32,2,512]{2,1,0:T(2,128)S(1)}, f32[32,2,512]{2,1,0:T(2,128)}, u32[]{:S(2)}, u32[]{:S(2)}) collective-permute-start(f32[32,2,512]{2,1,0:T(2,128)S(1)} %get-tuple-element.11), channel_id=1, source_target_pairs={{1,0},{2,1},{3,2},{4,3},{5,4},{6,5},{7,6},{0,7},{9,8},{10,9},{11,1... | collective-permute-start | bytes 393224 | tf_op jit(solution)/shard_map/ppermute | solution.py:20
  68.7 3.4 %copy-start.1 = (f32[512,256]{1,0:T(8,128)S(1)}, f32[512,256]{1,0:T(8,128)}, u32[]{:S(2)}) copy-start(f32[512,256]{1,0:T(8,128)} %copy-done) | copy-start | bytes 1572868
  68.7 3.4 %copy-start.3 = (f32[512,256,1]{1,0,2:T(8,128)S(1)}, f32[512,256,1]{1,0,2:T(8,128)}, u32[]{:S(2)}) copy-start(f32[512,256,1]{1,0,2:T(8,128)} %fusion.38) | copy-start | bytes 1572868
  70.7 1.5 %copy-start.7 = (f32[1,2,2,128]{3,2,1,0:T(2,128)S(1)}, f32[1,2,2,128]{3,2,1,0:T(2,128)}, u32[]{:S(2)}) copy-start(f32[1,2,2,128]{3,2,1,0:T(2,128)} %get-tuple-element.25) | copy-start | bytes 6148
  70.7 2.1 %copy-start.6 = (f32[1,2,2,128]{3,2,1,0:T(2,128)S(1)}, f32[1,2,2,128]{3,2,1,0:T(2,128)}, u32[]{:S(2)}) copy-start(f32[1,2,2,128]{3,2,1,0:T(2,128)} %get-tuple-element.26) | copy-start | bytes 6148
  70.7 2.6 %copy-start.5 = (f32[1,2,2,128]{3,2,1,0:T(2,128)S(1)}, f32[1,2,2,128]{3,2,1,0:T(2,128)}, u32[]{:S(2)}) copy-start(f32[1,2,2,128]{3,2,1,0:T(2,128)} %get-tuple-element.23) | copy-start | bytes 6148
  70.8 3.2 %copy-start.4 = (f32[1,2,2,128]{3,2,1,0:T(2,128)S(1)}, f32[1,2,2,128]{3,2,1,0:T(2,128)}, u32[]{:S(2)}) copy-start(f32[1,2,2,128]{3,2,1,0:T(2,128)} %get-tuple-element.24) | copy-start | bytes 6148
  70.9 7.5 %collective-permute-start.7 = (f32[32,2,512]{2,1,0:T(2,128)S(1)}, f32[32,2,512]{2,1,0:T(2,128)S(1)}, u32[]{:S(2)}, u32[]{:S(2)}) collective-permute-start(f32[32,2,512]{2,1,0:T(2,128)S(1)} %get-tuple-element.8), channel_id=1, source_target_pairs={{1,0},{2,1},{3,2},{4,3},{5,4},{6,5},{7,6},{0,7},{9,8},{10,9},{11,1... | collective-permute-start | bytes 393224 | tf_op jit(solution)/shard_map/ppermute | solution.py:20
  72.1 6.3 %collective-permute-start.6 = (f32[32,2,512]{2,1,0:T(2,128)S(1)}, f32[32,2,512]{2,1,0:T(2,128)}, u32[]{:S(2)}, u32[]{:S(2)}) collective-permute-start(f32[32,2,512]{2,1,0:T(2,128)S(1)} %get-tuple-element.9), channel_id=1, source_target_pairs={{0,1},{1,2},{2,3},{3,4},{4,5},{5,6},{6,7},{7,0},{8,9},{9,10},{10,1... | collective-permute-start | bytes 393224 | tf_op jit(solution)/shard_map/ppermute | solution.py:19
  81.9 2.6 %copy-start.8 = (f32[1,2,2,128]{3,1,2,0:T(2,128)S(1)}, f32[1,2,2,128]{3,1,2,0:T(2,128)}, u32[]{:S(2)}) copy-start(f32[1,2,2,128]{3,1,2,0:T(2,128)} %copy.18) | copy-start | bytes 6148
  81.9 2.6 %copy-start.9 = (f32[1,2,2,128]{3,1,2,0:T(2,128)S(1)}, f32[1,2,2,128]{3,1,2,0:T(2,128)}, u32[]{:S(2)}) copy-start(f32[1,2,2,128]{3,1,2,0:T(2,128)} %copy.17) | copy-start | bytes 6148
  81.9 2.5 %copy-start.10 = (f32[1,2,2,128]{3,1,2,0:T(2,128)S(1)}, f32[1,2,2,128]{3,1,2,0:T(2,128)}, u32[]{:S(2)}) copy-start(f32[1,2,2,128]{3,1,2,0:T(2,128)} %copy.20) | copy-start | bytes 6148
  81.9 2.5 %copy-start.11 = (f32[1,2,2,128]{3,1,2,0:T(2,128)S(1)}, f32[1,2,2,128]{3,1,2,0:T(2,128)}, u32[]{:S(2)}) copy-start(f32[1,2,2,128]{3,1,2,0:T(2,128)} %copy.19) | copy-start | bytes 6148
  82.0 2.5 %copy-start.12 = (s32[512]{0:T(512)S(1)}, s32[512]{0:T(512)}, u32[]{:S(2)}) copy-start(s32[512]{0:T(512)} %add_select_fusion) | copy-start | bytes 6148
  84.5 7.9 %copy-start.14 = (s32[1,1,2]{2,1,0:T(1,128)S(1)}, s32[1,1,2]{2,1,0:T(1,128)}, u32[]{:S(2)}) copy-start(s32[1,1,2]{2,1,0:T(1,128)} %param.5) | copy-start | bytes 28
where the time goes:
time: 132 us
  local copies, waits for them, and re-layouts  55.9 us (42%)
  blocking collectives  39.4 us (30%)
  starting transfers between devices  11.2 us (8%)
  other arithmetic  10.8 us (8%)
  matrix products  7.52 us (6%)
  waiting for transfers between devices  6.19 us (5%)
    psum x1, blocking collectives, shards(): group_mass = lax.psum(partial_mass, ('row', 'col'))  39.4 us
    slice x1, local copies, waits for them, and re-layouts, depth_table(): odds_half = lax.slice_in_dim(ident, 1, size_z, stride=2, axis=1)  19.5 us
    slice x1, local copies, waits for them, and re-layouts, depth_table(): evens_half = lax.slice_in_dim(ident, 0, size_z, stride=2, axis=1)  19.5 us
    ppermute x4, starting transfers between devices, extended(): after = lax.ppermute(initial, axis, down)  7.96 us
    dot_general x1, matrix products, shards(): jnp.dot(signal.reshape(size_x * size_y, size_z), table, precision=lax.Pre...  7.33 us
    slice x3, local copies, waits for them, and re-layouts, parity_part(): return lax.slice_in_dim(signal, which, length, stride=2, axis=axis_pos)  4.62 us
    unnamed x36, local copies, waits for them, and re-layouts  4.38 us
    ppermute x4, starting transfers between devices, extended(): before = lax.ppermute(last, axis, up)  3.23 us
  transfers between devices with their start and end apart: 8, of which 2 were waited for; matrix products, arithmetic and copies ran while one was open for 41% of the time, Pallas kernels for 0%

commit v1 on v0

v1 whole, which is shorter than its diff:
```python
import functools

import jax
import jax.numpy as jnp
import numpy as np
from jax import lax
from jax.experimental import pallas as pl
from jax.experimental.pallas import tpu as pltpu
from jax.sharding import PartitionSpec as P

GROUPS = 16
LEVELS = (0.25, 0.5, 1.0, 2.0)
MESH = pl.DeviceIdType.MESH
F32, BF16 = jnp.float32, jnp.bfloat16


def cyclic_matrix(n):
    half = n // 2
    ev, od = np.eye(n)[0::2], np.eye(n)[1::2]
    r = lambda a, k: np.roll(a, k, 0)
    d = od - (0.5625 * (ev + r(ev, -1)) - 0.0625 * (r(ev, 1) + r(ev, -2)))
    s = ev + (0.28125 * (r(d, 1) + d) - 0.03125 * (r(d, 2) + r(d, -1)))
    return np.stack([s, d], 1).reshape(n, n) if half else None


def local_matrix(n):
    half = n // 2
    t = np.eye(n + 6)
    v, (a, b, c, f0, f1, g) = t[:n], t[n:]
    e = {j: v[2 * j] for j in range(half)}
    o = {j: v[2 * j + 1] for j in range(half)}
    e[-1], e[half], e[half + 1] = a, f0, f1
    d = {
        j: o[j] - 0.5625 * (e[j] + e[j + 1]) + 0.0625 * (e[j - 1] + e[j + 2])
        for j in range(half)
    }
    d[-1] = b - 0.5625 * e[0] + 0.0625 * e[1]
    d[-2] = c + 0.0625 * e[0]
    d[half] = g + 0.0625 * e[half - 1]
    out = np.zeros((n, n + 6))
    for j in range(half):
        out[2 * j] = e[j] + 0.28125 * (d[j - 1] + d[j]) - 0.03125 * (d[j - 2] + d[j + 1])
        out[2 * j + 1] = d[j]
    return out


def partials_low(row, n):
    a = row(n - 2)
    b = row(n - 1) - 0.5625 * a + 0.0625 * row(n - 4)
    c = row(n - 3) - 0.5625 * (row(n - 4) + a) + 0.0625 * row(n - 6)
    return a, b, c


def partials_high(row):
    f0, f1 = row(0), row(2)
    return f0, f1, row(1) - 0.5625 * (f0 + f1) + 0.0625 * row(4)


def split(value):
    hi = value.astype(BF16)
    return hi, (value - hi.astype(F32)).astype(BF16)


def dot2(left, right):
    dot = functools.partial(jnp.dot, preferred_element_type=F32)
    if left.dtype == BF16:
        hi, lo = split(right)
        return dot(left, hi) + dot(left, lo)
    hi, lo = split(left)
    return dot(hi, right) + dot(lo, right)


def kernel(
    n_row, n_col, grp, cut_ref, map_ref, p_ref, ws_ref, wy_ref, wu_ref, wx_ref, wc_ref, wz_ref,
    out_ref, mass_ref,
    ext, q, sx, su, u, sc, cb, part, slots,
    in_sem, h_send, h_recv, g_send, g_recv,
):
    nx, ny, nz = p_ref.shape
    devices = n_row * n_col
    row, col = lax.axis_index("row"), lax.axis_index("col")
    me = row * n_col + col
    up_r, dn_r = lax.rem(row + 1, n_row), lax.rem(row + n_row - 1, n_row)
    up_c, dn_c = lax.rem(col + 1, n_col), lax.rem(col + n_col - 1, n_col)

    pieces = ((0, 8), (nx - 8, 8), (8, nx - 16))
    loads = []
    for i, (at, size) in enumerate(pieces):
        load = pltpu.make_async_copy(
            p_ref.at[pl.ds(at, size)], ext.at[pl.ds(at, size)], in_sem.at[i]
        )
        load.start()
        loads.append(load)

    def place(k):
        t = lax.rem(me + k, devices)
        return (t // n_col, lax.rem(t, n_col))

    barrier = pltpu.get_barrier_semaphore()

    @pl.loop(1, devices)
    def _(k):
        pl.semaphore_signal(barrier, inc=1, device_id=place(k), device_id_type=MESH)

    sends = []

    def send(src, dst, to):
        i = len(sends)
        copy = pltpu.make_async_remote_copy(
            src_ref=src, dst_ref=dst, send_sem=h_send.at[i], recv_sem=h_recv.at[i],
            device_id=to, device_id_type=MESH,
        )
        copy.start()
        sends.append(copy)

    loads[0].wait()
    loads[1].wait()
    _, b, c = partials_low(lambda i: ext[i], nx)
    sx[0], sx[1] = b, c
    sx[2] = partials_high(lambda i: ext[i])[2]
    loads[2].wait()
    for g in range(nx // grp):
        at = pl.ds(g * grp, grp)
        got = dot2(ws_ref[...], ext[at].reshape(grp * ny, nz))
        su[:, at, :] = got.reshape(6, grp, nz)
    sc[...] = jnp.zeros_like(sc)
    for d in range(4):
        for k in range(3):
            plane = (d % 2) * 3 + k
            x_row = lambda i: su[plane, pl.ds(i, 1), :]
            got = partials_low(x_row, nx) if d < 2 else partials_high(x_row)
            for i in range(3):
                sc[d, pl.ds(3 * i + k, 1), :] = got[i]

    pl.semaphore_wait(barrier, devices - 1)
    send(ext.at[nx - 2], ext.at[nx], (up_r, col))
    send(ext.at[0], ext.at[nx + 3], (dn_r, col))
    send(ext.at[2], ext.at[nx + 4], (dn_r, col))
    send(su.at[pl.ds(0, 3)], u.at[pl.ds(0, 3)], (row, up_c))
    send(su.at[pl.ds(3, 3)], u.at[pl.ds(3, 3)], (row, dn_c))
    send(sx.at[pl.ds(0, 2)], ext.at[pl.ds(nx + 1, 2)], (up_r, col))
    send(sx.at[2], ext.at[nx + 5], (dn_r, col))
    for d in range(4):
        to = (up_r if d < 2 else dn_r, up_c if d % 2 == 0 else dn_c)
        send(sc.at[d], cb.at[d], to)

    for g in range(nx // grp):
        at = pl.ds(g * grp, grp)
        q[at] = dot2(wy_ref[...], ext[at].reshape(grp * ny, nz)).reshape(grp, ny, nz)
    for copy in sends:
        copy.wait_recv()
    for g in range(nx // grp):
        at = pl.ds(g * grp, grp)
        more = dot2(wu_ref[...], u[:, at, :].reshape(6 * grp, nz))
        q[at] += more.reshape(grp, ny, nz)
    edge = dot2(wx_ref[...], ext[pl.ds(nx, 6)].reshape(6 * ny, nz))
    edge += dot2(wc_ref[...], cb[...].reshape(-1, nz))
    q[pl.ds(nx, 6)] = edge.reshape(6, ny, nz)

    for copy in sends:
        copy.wait_send()
    half = nx // 2

    @pl.loop(0, ny // 8)
    def _(t):
        rows = pl.ds(pl.multiple_of(t * 8, 8), 8)
        e = {j: q[2 * j, rows, :] for j in range(-0, half)}
        o = lambda j: q[2 * j + 1, rows, :]
        e[-1], e[half], e[half + 1] = (q[nx + i, rows, :] for i in (0, 3, 4))
        d = {
            -1: q[nx + 1, rows, :] - 0.5625 * e[0] + 0.0625 * e[1],
            -2: q[nx + 2, rows, :] + 0.0625 * e[0],
        }

        def detail(j):
            if j == half:
                return q[nx + 5, rows, :] + 0.0625 * e[half - 1]
            return o(j) - 0.5625 * (e[j] + e[j + 1]) + 0.0625 * (e[j - 1] + e[j + 2])

        d[0] = detail(0)
        for j in range(half):
            d[j + 1] = detail(j + 1)
            smooth = e[j] + 0.28125 * (d[j - 1] + d[j]) - 0.03125 * (d[j - 2] + d[j + 1])
            ext[2 * j, rows, :] = smooth
            ext[2 * j + 1, rows, :] = d[j]

    zb = cut_ref.shape[2]
    width = nz // zb
    cuts = jnp.concatenate(
        [jnp.full((1, width), -cut_ref[0, 0, z], jnp.int32) for z in range(zb)], 1
    )
    scale = jnp.exp2(cuts.astype(F32))
    limits = [level * scale for level in LEVELS]
    odd = lambda axis: lax.broadcasted_iota(jnp.int32, (8, nz), axis) % 2
    mixed = (odd(0) + odd(1)) > 0

    def z_group(g, totals):
        at = pl.ds(g * grp, grp)
        made = dot2(ext[at].reshape(grp * ny, nz), wz_ref[...])
        out_ref[at] = made.reshape(grp, ny, nz)
        totals = list(totals)
        for i in range(grp * ny // 8):
            size = jnp.abs(made[8 * i : 8 * i + 8])
            if (8 * i // ny) % 2 == 0:
                size = jnp.where(mixed, size, 0.0)
            for n, limit in enumerate(limits):
                totals[n] += jnp.maximum(size - limit, 0.0)
        return tuple(totals)

    totals = lax.fori_loop(
        0, nx // grp, z_group, tuple(jnp.zeros((8, nz), F32) for _ in LEVELS)
    )
    lane = lax.broadcasted_iota(jnp.int32, (1, 128), 1)
    line = jnp.zeros((1, 128), F32)
    cells = nx * ny * width
    n_lev = len(LEVELS)
    for z in range(zb):
        for n in range(n_lev):
            mass = jnp.sum(totals[n][:, z * width : (z + 1) * width], keepdims=True) / cells
            line += jnp.where(lane == map_ref[0, 0, z] * n_lev + n, mass, 0.0)
    part[...] = line
    slots[me] = line

    def spread(k):
        t = lax.rem(me + k, devices)
        return pltpu.make_async_remote_copy(
            src_ref=part, dst_ref=slots.at[me], send_sem=g_send.at[t],
            recv_sem=g_recv.at[me], device_id=place(k), device_id_type=MESH,
        )

    @pl.loop(1, devices)
    def _(k):
        spread(k).start()

    @pl.loop(1, devices)
    def _(k):
        t = lax.rem(me + k, devices)
        pltpu.make_async_remote_copy(
            src_ref=part, dst_ref=slots.at[t], send_sem=g_send.at[t],
            recv_sem=g_recv.at[t], device_id=place(k), device_id_type=MESH,
        ).wait()

    total = jnp.sum(slots[...], axis=0)
    wide = jnp.broadcast_to(total, (GROUPS, 128))
    at_row = lax.broadcasted_iota(jnp.int32, (GROUPS, 128), 0)
    at_lane = lax.broadcasted_iota(jnp.int32, (GROUPS, 128), 1)
    at_col = lax.broadcasted_iota(jnp.int32, (GROUPS, n_lev), 1)
    result = jnp.zeros((GROUPS, n_lev), F32)
    for n in range(n_lev):
        pick = jnp.where(at_lane == at_row * n_lev + n, wide, 0.0)
        result = jnp.where(at_col == n, jnp.sum(pick, axis=1, keepdims=True), result)
    mass_ref[...] = result


def solution(mesh):
    n_row, n_col = mesh.shape["row"], mesh.shape["col"]

    def shards(pressure, cut_exponent, group_map):
        nx, ny, nz = pressure.shape
        grp = 8
        devices = n_row * n_col
        local = local_matrix(ny)
        wy = np.kron(np.eye(grp), local[:, :ny])
        wu = np.einsum("xw,yk->xykw", np.eye(grp), local[:, ny:]).reshape(grp * ny, 6 * grp)
        eye = np.eye(ny)
        row = lambda i: eye[i]
        near = np.stack(partials_low(row, ny) + partials_high(row))
        ws = np.einsum("ky,xw->kxwy", near, np.eye(grp)).reshape(6 * grp, grp * ny)
        wx = np.kron(np.eye(6), local[:, :ny])
        wc = np.zeros((6, ny, 4, 16))
        for d in range(4):
            for i in range(3):
                for k in range(3):
                    wc[(d // 2) * 3 + i, :, d, 3 * i + k] = local[:, ny + (d % 2) * 3 + k]
        wc = wc.reshape(6 * ny, 64)
        weights = [jnp.asarray(w, BF16) for w in (ws, wy, wu, wx, wc, cyclic_matrix(nz).T)]
        vmem = pl.BlockSpec(memory_space=pltpu.VMEM)
        smem = pl.BlockSpec(memory_space=pltpu.SMEM)
        return pl.pallas_call(
            functools.partial(kernel, n_row, n_col, grp),
            out_shape=(
                jax.ShapeDtypeStruct((nx, ny, nz), F32),
                jax.ShapeDtypeStruct((GROUPS, len(LEVELS)), F32),
            ),
            in_specs=[smem, smem, pl.BlockSpec(memory_space=pltpu.HBM)] + [vmem] * 6,
            out_specs=(vmem, vmem),
            scratch_shapes=[
                pltpu.VMEM((nx + 8, ny, nz), F32),
                pltpu.VMEM((nx + 6, ny, nz), F32),
                pltpu.VMEM((3, ny, nz), F32),
                pltpu.VMEM((6, nx, nz), F32),
                pltpu.VMEM((6, nx, nz), F32),
                pltpu.VMEM((4, 16, nz), F32),
                pltpu.VMEM((4, 16, nz), F32),
                pltpu.VMEM((1, 128), F32),
                pltpu.VMEM((devices, 1, 128), F32),
                pltpu.SemaphoreType.DMA((3,)),
                pltpu.SemaphoreType.DMA((11,)),
                pltpu.SemaphoreType.DMA((11,)),
                pltpu.SemaphoreType.DMA((devices,)),
                pltpu.SemaphoreType.DMA((devices,)),
            ],
            compiler_params=pltpu.CompilerParams(
                collective_id=0, has_side_effects=True, vmem_limit_bytes=28 * 2**20
            ),
        )(cut_exponent, group_map, pressure, *weights)

    specs = P("row", "col", None)
    return jax.shard_map(
        shards, mesh=mesh, in_specs=(specs,) * 3, out_specs=(specs, P()), check_vma=False
    )
```

time: 132 us -> 42.3 us (0.32)
  local copies, waits for them, and re-layouts: 55.9 us -> 10.1 us
  blocking collectives: 39.4 us -> 0 us
  Pallas kernels: 0 us -> 31.2 us
  starting transfers between devices: 11.2 us -> 0 us
  other arithmetic: 10.8 us -> 0 us
  matrix products: 7.52 us -> 0 us
  waiting for transfers between devices: 6.19 us -> 0 us
    slice x11 -> x0, local copies, waits for them, and re-layouts: 44.1 us -> none  [the longest x1 19.5 us: depth_table(): odds_half = lax.slice_in_dim(ident, 1, size_z, stride=2, axis=1)]
    psum x1 -> x0, blocking collectives: 39.4 us -> none  [shards(): group_mass = lax.psum(partial_mass, ('row', 'col'))]
    pallas_call x0 -> x1, Pallas kernels: none -> 31.2 us  [shards(): pl.pallas_call(functools.partial(kernel, n_row, n_col, grp), out_shape=(j...]
    ppermute x8 -> x0, starting transfers between devices: 11.2 us -> none  [the longest x4 7.96 us: extended(): after = lax.ppermute(initial, axis, down)]
    dot_general x2 -> x0, matrix products: 7.52 us -> none  [the longest x1 7.33 us: shards(): jnp.dot(signal.reshape(size_x * size_y, size_z), table, precision=lax.Pre...]
    ppermute x8 -> x0, waiting for transfers between devices: 6.19 us -> none  [the longest x4 3.12 us: extended(): before = lax.ppermute(last, axis, up)]
    unnamed x36 -> x19, local copies, waits for them, and re-layouts: 4.38 us -> 9.42 us
    sub x3 -> x0, other arithmetic: 3.96 us -> none  [the longest x1 1.99 us: shards(): detail = odds_half - predict_odd(padded, 1, 1, half)]
  transfers between devices with their start and end apart: 8 -> 0, of which waited for: 2 -> 0; matrix products, arithmetic and copies ran while one was open for 41% -> 0% of each run, Pallas kernels for 0% -> 0%
where the time goes in v1:
time: 42.3 us; the launch traced here: 41.9 us
  Pallas kernels  31.2 us (74%)
  local copies, waits for them, and re-layouts  10.1 us (24%)
  between operations  0.66 us (2%)
    pallas_call x1, Pallas kernels, shards(): pl.pallas_call(functools.partial(kernel, n_row, n_col, grp), out_shape=(j...  31.2 us
    unnamed x19, local copies, waits for them, and re-layouts  9.42 us

profile of v1, /device:TPU:0, one launch (start us, length us, event | category | flops | bytes accessed | tf_op | source)
XLA Modules:
  0.0 41.9 jit_solution(14300586530304661228)
XLA Ops:
  0.6 0.0 copy-start
  0.6 1.6 %copy-done = f32[32,32,512]{2,1,0:T(8,128)S(1)} copy-done((f32[32,32,512]{2,1,0:T(8,128)S(1)}, f32[32,32,512]{2,1,0:T(8,128)}, u32[]{:S(2)}) %copy-start) | copy-done | bytes 2097176
  2.2 0.0 copy-start.1
  2.2 1.0 %copy-done.1 = bf16[512,512]{1,0:T(8,128)(2,1)S(1)} copy-done((bf16[512,512]{1,0:T(8,128)(2,1)S(1)}, bf16[512,512]{1,0:T(8,128)(2,1)}, u32[]{:S(2)}) %copy-start.1) | copy-done | bytes 524312
  3.3 0.0 copy-start.2
  3.3 0.9 %copy-done.2 = bf16[256,256]{1,0:T(8,128)(2,1)S(1)} copy-done((bf16[256,256]{1,0:T(8,128)(2,1)S(1)}, bf16[256,256]{1,0:T(8,128)(2,1)}, u32[]{:S(2)}) %copy-start.2) | copy-done | bytes 131096
  4.2 0.0 copy-start.3
  4.2 0.9 %copy-done.3 = bf16[192,192]{1,0:T(8,128)(2,1)S(1)} copy-done((bf16[192,192]{1,0:T(8,128)(2,1)S(1)}, bf16[192,192]{1,0:T(8,128)(2,1)}, u32[]{:S(2)}) %copy-start.3) | copy-done | bytes 73752
  5.1 0.0 copy-start.4
  5.1 0.8 %copy-done.4 = bf16[256,48]{1,0:T(8,128)(2,1)S(1)} copy-done((bf16[256,48]{1,0:T(8,128)(2,1)S(1)}, bf16[256,48]{1,0:T(8,128)(2,1)}, u32[]{:S(2)}) %copy-start.4) | copy-done | bytes 24600
  5.9 0.0 copy-start.5
  5.9 0.8 %copy-done.5 = bf16[192,64]{1,0:T(8,128)(2,1)S(1)} copy-done((bf16[192,64]{1,0:T(8,128)(2,1)S(1)}, bf16[192,64]{1,0:T(8,128)(2,1)}, u32[]{:S(2)}) %copy-start.5) | copy-done | bytes 24600
  6.7 0.0 copy-start.6
  6.7 0.7 %copy-done.6 = bf16[48,256]{1,0:T(8,128)(2,1)S(1)} copy-done((bf16[48,256]{1,0:T(8,128)(2,1)S(1)}, bf16[48,256]{1,0:T(8,128)(2,1)}, u32[]{:S(2)}) %copy-start.6) | copy-done | bytes 24600
  7.4 0.0 copy-start.7
  7.4 0.7 %copy-done.7 = s32[1,1,2]{2,1,0:T(1,128)S(1)} copy-done((s32[1,1,2]{2,1,0:T(1,128)S(1)}, s32[1,1,2]{2,1,0:T(1,128)}, u32[]{:S(2)}) %copy-start.7) | copy-done | bytes 32
  8.1 0.0 copy-start.8
  8.1 0.7 %copy-done.8 = s32[1,1,2]{2,1,0:T(1,128)S(1)} copy-done((s32[1,1,2]{2,1,0:T(1,128)S(1)}, s32[1,1,2]{2,1,0:T(1,128)}, u32[]{:S(2)}) %copy-start.8) | copy-done | bytes 32
  8.8 31.2 %shard_map.104 = (f32[32,32,512]{2,1,0:T(8,128)S(1)}, f32[16,4]{1,0:T(8,128)S(1)}) custom-call(s32[1,1,2]{2,1,0:T(1,128)S(1)} %copy-done.7, s32[1,1,2]{2,1,0:T(1,128)S(1)} %copy-done.8, f32[32,32,512]{2,1,0:T(8,128)S(1)} %copy-done, bf16[48,256]{1,0:T(8,128)(2,1)S(1)} %copy-done.6, bf16[256,256]{1,0:T(8,128)(2,1)S(1)} %copy-done.2, ...), custom_call_target="tpu_custom_call" | custom-call | tf_op jit(solution)/shard_map/pallas_call | solution.py:279
  39.9 0.7 %copy.11 = f32[16,4]{0,1:T(4,128)} copy(f32[16,4]{1,0:T(8,128)S(1)} %get-tuple-element.3) | data formatting | bytes 512 | tf_op jit(solution)/shard_map/pallas_call | solution.py:279
  40.6 1.3 %copy.13 = f32[32,32,512]{2,1,0:T(8,128)} copy(f32[32,32,512]{2,1,0:T(8,128)S(1)} %get-tuple-element.6) | data formatting | bytes 4194304
Async XLA Ops:
  0.6 1.6 %copy-start = (f32[32,32,512]{2,1,0:T(8,128)S(1)}, f32[32,32,512]{2,1,0:T(8,128)}, u32[]{:S(2)}) copy-start(f32[32,32,512]{2,1,0:T(8,128)} %p_ref.1) | copy-start | bytes 6291460
  2.2 1.0 %copy-start.1 = (bf16[512,512]{1,0:T(8,128)(2,1)S(1)}, bf16[512,512]{1,0:T(8,128)(2,1)}, u32[]{:S(2)}) copy-start(bf16[512,512]{1,0:T(8,128)(2,1)} %constant.17.clone.wz_ref) | copy-start | bytes 1572868
  3.3 0.9 %copy-start.2 = (bf16[256,256]{1,0:T(8,128)(2,1)S(1)}, bf16[256,256]{1,0:T(8,128)(2,1)}, u32[]{:S(2)}) copy-start(bf16[256,256]{1,0:T(8,128)(2,1)} %constant.13.clone.wy_ref) | copy-start | bytes 393220
  4.2 0.9 %copy-start.3 = (bf16[192,192]{1,0:T(8,128)(2,1)S(1)}, bf16[192,192]{1,0:T(8,128)(2,1)}, u32[]{:S(2)}) copy-start(bf16[192,192]{1,0:T(8,128)(2,1)} %constant.15.clone.wx_ref) | copy-start | bytes 221188
  5.1 0.8 %copy-start.4 = (bf16[256,48]{1,0:T(8,128)(2,1)S(1)}, bf16[256,48]{1,0:T(8,128)(2,1)}, u32[]{:S(2)}) copy-start(bf16[256,48]{1,0:T(8,128)(2,1)} %constant.14.clone.wu_ref) | copy-start | bytes 73732
  5.9 0.8 %copy-start.5 = (bf16[192,64]{1,0:T(8,128)(2,1)S(1)}, bf16[192,64]{1,0:T(8,128)(2,1)}, u32[]{:S(2)}) copy-start(bf16[192,64]{1,0:T(8,128)(2,1)} %constant.16.clone.wc_ref) | copy-start | bytes 73732
  6.7 0.7 %copy-start.6 = (bf16[48,256]{1,0:T(8,128)(2,1)S(1)}, bf16[48,256]{1,0:T(8,128)(2,1)}, u32[]{:S(2)}) copy-start(bf16[48,256]{1,0:T(8,128)(2,1)} %constant.12.clone.ws_ref) | copy-start | bytes 73732
  7.4 0.7 %copy-start.7 = (s32[1,1,2]{2,1,0:T(1,128)S(1)}, s32[1,1,2]{2,1,0:T(1,128)}, u32[]{:S(2)}) copy-start(s32[1,1,2]{2,1,0:T(1,128)} %cut_ref.1) | copy-start | bytes 28
  8.1 0.7 %copy-start.8 = (s32[1,1,2]{2,1,0:T(1,128)S(1)}, s32[1,1,2]{2,1,0:T(1,128)}, u32[]{:S(2)}) copy-start(s32[1,1,2]{2,1,0:T(1,128)} %map_ref.1) | copy-start | bytes 28

commit v2 on v1

--- a/solution.py
+++ b/solution.py
@@ -71,11 +71,14 @@
 
 
 def kernel(
-    n_row, n_col, grp, cut_ref, map_ref, p_ref, ws_ref, wy_ref, wu_ref, wx_ref, wc_ref, wz_ref,
-    out_ref, mass_ref,
-    ext, q, sx, su, u, sc, cb, part, slots,
-    in_sem, h_send, h_recv, g_send, g_recv,
+    n_row, n_col, grp, cut_hbm, map_hbm, p_ref, *refs
 ):
+    weights, refs = refs[:6], refs[6:]
+    out_hbm, mass_ref = refs[:2]
+    ext, q, sx, su, u, sc, cb, part, slots, out_ref, cut_ref, map_ref = refs[2:14]
+    held = refs[14:20]
+    ws_ref, wy_ref, wu_ref, wx_ref, wc_ref, wz_ref = held
+    in_sem, o_sem, w_sem, h_send, h_recv, g_send, g_recv = refs[20:]
     nx, ny, nz = p_ref.shape
     devices = n_row * n_col
     row, col = lax.axis_index("row"), lax.axis_index("col")
@@ -92,6 +95,14 @@
         load.start()
         loads.append(load)
 
+    fetched = []
+    for i, (src, dst) in enumerate(
+        zip((*weights, cut_hbm, map_hbm), (*held, cut_ref, map_ref), strict=True)
+    ):
+        fetch = pltpu.make_async_copy(src, dst, w_sem.at[i])
+        fetch.start()
+        fetched.append(fetch)
+
     def place(k):
         t = lax.rem(me + k, devices)
         return (t // n_col, lax.rem(t, n_col))
@@ -118,71 +129,68 @@
     _, b, c = partials_low(lambda i: ext[i], nx)
     sx[0], sx[1] = b, c
     sx[2] = partials_high(lambda i: ext[i])[2]
+    pl.semaphore_wait(barrier, devices - 1)
+    send(sx.at[pl.ds(0, 2)], ext.at[pl.ds(nx + 1, 2)], (up_r, col))
+    send(sx.at[2], ext.at[nx + 5], (dn_r, col))
+    send(ext.at[nx - 2], ext.at[nx], (up_r, col))
+    send(ext.at[0], ext.at[nx + 3], (dn_r, col))
+    send(ext.at[2], ext.at[nx + 4], (dn_r, col))
     loads[2].wait()
+    for fetch in fetched:
+        fetch.wait()
     for g in range(nx // grp):
         at = pl.ds(g * grp, grp)
         got = dot2(ws_ref[...], ext[at].reshape(grp * ny, nz))
         su[:, at, :] = got.reshape(6, grp, nz)
-    sc[...] = jnp.zeros_like(sc)
     for d in range(4):
         for k in range(3):
             plane = (d % 2) * 3 + k
             x_row = lambda i: su[plane, pl.ds(i, 1), :]
             got = partials_low(x_row, nx) if d < 2 else partials_high(x_row)
             for i in range(3):
-                sc[d, pl.ds(3 * i + k, 1), :] = got[i]
-
-    pl.semaphore_wait(barrier, devices - 1)
-    send(ext.at[nx - 2], ext.at[nx], (up_r, col))
-    send(ext.at[0], ext.at[nx + 3], (dn_r, col))
-    send(ext.at[2], ext.at[nx + 4], (dn_r, col))
+                sc[9 * d + 3 * i + k] = got[i]
+
     send(su.at[pl.ds(0, 3)], u.at[pl.ds(0, 3)], (row, up_c))
     send(su.at[pl.ds(3, 3)], u.at[pl.ds(3, 3)], (row, dn_c))
-    send(sx.at[pl.ds(0, 2)], ext.at[pl.ds(nx + 1, 2)], (up_r, col))
-    send(sx.at[2], ext.at[nx + 5], (dn_r, col))
     for d in range(4):
         to = (up_r if d < 2 else dn_r, up_c if d % 2 == 0 else dn_c)
-        send(sc.at[d], cb.at[d], to)
+        send(sc.at[pl.ds(9 * d, 9)], cb.at[pl.ds(9 * d, 9)], to)
 
     for g in range(nx // grp):
         at = pl.ds(g * grp, grp)
         q[at] = dot2(wy_ref[...], ext[at].reshape(grp * ny, nz)).reshape(grp, ny, nz)
-    for copy in sends:
+    for copy in sends[5:7]:
         copy.wait_recv()
     for g in range(nx // grp):
         at = pl.ds(g * grp, grp)
         more = dot2(wu_ref[...], u[:, at, :].reshape(6 * grp, nz))
         q[at] += more.reshape(grp, ny, nz)
-    edge = dot2(wx_ref[...], ext[pl.ds(nx, 6)].reshape(6 * ny, nz))
-    edge += dot2(wc_ref[...], cb[...].reshape(-1, nz))
-    q[pl.ds(nx, 6)] = edge.reshape(6, ny, nz)
-
-    for copy in sends:
-        copy.wait_send()
     half = nx // 2
 
-    @pl.loop(0, ny // 8)
-    def _(t):
-        rows = pl.ds(pl.multiple_of(t * 8, 8), 8)
-        e = {j: q[2 * j, rows, :] for j in range(-0, half)}
-        o = lambda j: q[2 * j + 1, rows, :]
-        e[-1], e[half], e[half + 1] = (q[nx + i, rows, :] for i in (0, 3, 4))
-        d = {
-            -1: q[nx + 1, rows, :] - 0.5625 * e[0] + 0.0625 * e[1],
-            -2: q[nx + 2, rows, :] + 0.0625 * e[0],
-        }
-
-        def detail(j):
-            if j == half:
-                return q[nx + 5, rows, :] + 0.0625 * e[half - 1]
-            return o(j) - 0.5625 * (e[j] + e[j + 1]) + 0.0625 * (e[j - 1] + e[j + 2])
-
-        d[0] = detail(0)
-        for j in range(half):
-            d[j + 1] = detail(j + 1)
-            smooth = e[j] + 0.28125 * (d[j - 1] + d[j]) - 0.03125 * (d[j - 2] + d[j + 1])
-            ext[2 * j, rows, :] = smooth
-            ext[2 * j + 1, rows, :] = d[j]
+    def x_lift(low, high):
+        @pl.loop(0, ny // 8)
+        def _(t):
+            rows = pl.ds(pl.multiple_of(t * 8, 8), 8)
+            far = {-1: nx, half: nx + 3, half + 1: nx + 4}
+            first, last = max(low - 3, -1), min(high + 2, half + 1)
+            e = {j: q[far.get(j, 2 * j), rows, :] for j in range(first, last + 1)}
+
+            def detail(j):
+                if j == -1:
+                    return q[nx + 1, rows, :] - 0.5625 * e[0] + 0.0625 * e[1]
+                if j == -2:
+                    return q[nx + 2, rows, :] + 0.0625 * e[0]
+                if j == half:
+                    return q[nx + 5, rows, :] + 0.0625 * e[half - 1]
+                odd = q[2 * j + 1, rows, :]
+                return odd - 0.5625 * (e[j] + e[j + 1]) + 0.0625 * (e[j - 1] + e[j + 2])
+
+            d = {j: detail(j) for j in range(low - 2, low + 1)}
+            for j in range(low, high):
+                d[j + 1] = detail(j + 1)
+                near, wide = d[j - 1] + d[j], d[j - 2] + d[j + 1]
+                ext[2 * j, rows, :] = e[j] + 0.28125 * near - 0.03125 * wide
+                ext[2 * j + 1, rows, :] = d[j]
 
     zb = cut_ref.shape[2]
     width = nz // zb
@@ -198,6 +206,7 @@
         at = pl.ds(g * grp, grp)
         made = dot2(ext[at].reshape(grp * ny, nz), wz_ref[...])
         out_ref[at] = made.reshape(grp, ny, nz)
+        pltpu.make_async_copy(out_ref.at[at], out_hbm.at[at], o_sem.at[g]).start()
         totals = list(totals)
         for i in range(grp * ny // 8):
             size = jnp.abs(made[8 * i : 8 * i + 8])
@@ -207,9 +216,21 @@
                 totals[n] += jnp.maximum(size - limit, 0.0)
         return tuple(totals)
 
-    totals = lax.fori_loop(
-        0, nx // grp, z_group, tuple(jnp.zeros((8, nz), F32) for _ in LEVELS)
-    )
+    groups = nx // grp
+    totals = tuple(jnp.zeros((8, nz), F32) for _ in LEVELS)
+    x_lift(grp // 2, half - grp // 2)
+    totals = lax.fori_loop(1, groups - 1, z_group, totals)
+    for copy in sends[:5] + sends[7:]:
+        copy.wait_recv()
+    for copy in sends:
+        copy.wait_send()
+    edge = dot2(wx_ref[...], ext[pl.ds(nx, 6)].reshape(6 * ny, nz))
+    edge += dot2(wc_ref[...], cb[...].reshape(-1, nz))
+    q[pl.ds(nx, 6)] = edge.reshape(6, ny, nz)
+    x_lift(0, grp // 2)
+    x_lift(half - grp // 2, half)
+    for g in (0, groups - 1):
+        totals = z_group(g, totals)
     lane = lax.broadcasted_iota(jnp.int32, (1, 128), 1)
     line = jnp.zeros((1, 128), F32)
     cells = nx * ny * width
@@ -239,6 +260,10 @@
             src_ref=part, dst_ref=slots.at[t], send_sem=g_send.at[t],
             recv_sem=g_recv.at[t], device_id=place(k), device_id_type=MESH,
         ).wait()
+
+    for g in range(groups):
+        at = pl.ds(g * grp, grp)
+        pltpu.make_async_copy(out_ref.at[at], out_hbm.at[at], o_sem.at[g]).wait()
 
     total = jnp.sum(slots[...], axis=0)
     wide = jnp.broadcast_to(total, (GROUPS, 128))
@@ -267,41 +292,47 @@
         near = np.stack(partials_low(row, ny) + partials_high(row))
         ws = np.einsum("ky,xw->kxwy", near, np.eye(grp)).reshape(6 * grp, grp * ny)
         wx = np.kron(np.eye(6), local[:, :ny])
-        wc = np.zeros((6, ny, 4, 16))
+        wc = np.zeros((6, ny, 4, 9))
         for d in range(4):
             for i in range(3):
                 for k in range(3):
                     wc[(d // 2) * 3 + i, :, d, 3 * i + k] = local[:, ny + (d % 2) * 3 + k]
-        wc = wc.reshape(6 * ny, 64)
+        wc = wc.reshape(6 * ny, 36)
         weights = [jnp.asarray(w, BF16) for w in (ws, wy, wu, wx, wc, cyclic_matrix(nz).T)]
         vmem = pl.BlockSpec(memory_space=pltpu.VMEM)
-        smem = pl.BlockSpec(memory_space=pltpu.SMEM)
+        hbm = pl.BlockSpec(memory_space=pl.ANY)
         return pl.pallas_call(
             functools.partial(kernel, n_row, n_col, grp),
             out_shape=(
                 jax.ShapeDtypeStruct((nx, ny, nz), F32),
                 jax.ShapeDtypeStruct((GROUPS, len(LEVELS)), F32),
             ),
-            in_specs=[smem, smem, pl.BlockSpec(memory_space=pltpu.HBM)] + [vmem] * 6,
-            out_specs=(vmem, vmem),
+            in_specs=[hbm] * 9,
+            out_specs=(hbm, vmem),
             scratch_shapes=[
                 pltpu.VMEM((nx + 8, ny, nz), F32),
                 pltpu.VMEM((nx + 6, ny, nz), F32),
                 pltpu.VMEM((3, ny, nz), F32),
                 pltpu.VMEM((6, nx, nz), F32),
                 pltpu.VMEM((6, nx, nz), F32),
-                pltpu.VMEM((4, 16, nz), F32),
-                pltpu.VMEM((4, 16, nz), F32),
+                pltpu.VMEM((36, 1, nz), F32),
+                pltpu.VMEM((36, 1, nz), F32),
                 pltpu.VMEM((1, 128), F32),
                 pltpu.VMEM((devices, 1, 128), F32),
+                pltpu.VMEM((nx, ny, nz), F32),
+                pltpu.SMEM(cut_exponent.shape, jnp.int32),
+                pltpu.SMEM(group_map.shape, jnp.int32),
+                *(pltpu.VMEM(w.shape, BF16) for w in weights),
                 pltpu.SemaphoreType.DMA((3,)),
+                pltpu.SemaphoreType.DMA((nx // grp,)),
+                pltpu.SemaphoreType.DMA((8,)),
                 pltpu.SemaphoreType.DMA((11,)),
                 pltpu.SemaphoreType.DMA((11,)),
                 pltpu.SemaphoreType.DMA((devices,)),
                 pltpu.SemaphoreType.DMA((devices,)),
             ],
             compiler_params=pltpu.CompilerParams(
-                collective_id=0, has_side_effects=True, vmem_limit_bytes=28 * 2**20
+                collective_id=0, has_side_effects=True, vmem_limit_bytes=62 * 2**20
             ),
         )(cut_exponent, group_map, pressure, *weights)
 

time: 42.3 us -> 33.4 us (0.79)
  local copies, waits for them, and re-layouts: 10.1 us -> 4.53 us
  Pallas kernels: 31.2 us -> 28 us
    unnamed x19 -> x1, local copies, waits for them, and re-layouts: 9.42 us -> 3.18 us
    pallas_call x1, Pallas kernels: 31.2 us -> 28 us  [shards(): pl.pallas_call(functools.partial(kernel, n_row, n_col, grp), out_shape=(j...]
    pallas_call x1, local copies, waits for them, and re-layouts: 0.65 us -> 1.35 us  [shards(): pl.pallas_call(functools.partial(kernel, n_row, n_col, grp), out_shape=(j...]
where the time goes in v2:
time: 33.4 us; the launch traced here: 33.1 us
  Pallas kernels  28 us (84%)
  local copies, waits for them, and re-layouts  4.53 us (14%)
  between operations  0.64 us (2%)
    pallas_call x1, Pallas kernels, shards(): pl.pallas_call(functools.partial(kernel, n_row, n_col, grp), out_shape=(j...  28 us
    unnamed x1, local copies, waits for them, and re-layouts  3.18 us
    pallas_call x1, local copies, waits for them, and re-layouts, shards(): pl.pallas_call(functools.partial(kernel, n_row, n_col, grp), out_shape=(j...  1.35 us

profile of v2, /device:TPU:0, one launch (start us, length us, event | category | flops | bytes accessed | tf_op | source)
XLA Modules:
  0.0 33.1 jit_solution(2195225879616636493)
XLA Ops:
  0.6 28.0 %shard_map.104 = (f32[32,32,512]{2,1,0:T(8,128)}, f32[16,4]{1,0:T(8,128)}) custom-call(s32[1,1,2]{2,1,0:T(1,128)} %cut_hbm.1, s32[1,1,2]{2,1,0:T(1,128)} %map_hbm.1, f32[32,32,512]{2,1,0:T(8,128)} %p_ref.1, bf16[48,256]{1,0:T(8,128)(2,1)} %constant.12.clone.refs_0_, bf16[256,256]{1,0:T(8,128)(2,1)} %constant.13.clone.refs_1_, ...), custom_call_target="tpu_custom_call" | custom-call | tf_op jit(solution)/shard_map/pallas_call | solution.py:304
  28.6 1.3 %copy.11 = f32[16,4]{0,1:T(4,128)} copy(f32[16,4]{1,0:T(8,128)} %get-tuple-element.3) | data formatting | bytes 512 | tf_op jit(solution)/shard_map/pallas_call | solution.py:304
  29.9 3.2 %copy.13 = f32[32,32,512]{2,1,0:T(8,128)} copy(f32[32,32,512]{2,1,0:T(8,128)} %get-tuple-element.6) | data formatting | bytes 4194304

commit v3 on v2

--- a/solution.py
+++ b/solution.py
@@ -103,15 +103,28 @@
         fetch.start()
         fetched.append(fetch)
 
-    def place(k):
-        t = lax.rem(me + k, devices)
-        return (t // n_col, lax.rem(t, n_col))
+    def wrap(value, size):
+        return lax.select(value >= size, value - size, value)
+
+    def peers(visit):
+        @pl.loop(1, n_col)
+        def _(k):
+            visit(row, wrap(col + k, n_col))
+
+        @pl.loop(1, n_row)
+        def _(j):
+            other = wrap(row + j, n_row)
+
+            @pl.loop(0, n_col)
+            def _(k):
+                visit(other, wrap(col + k, n_col))
 
     barrier = pltpu.get_barrier_semaphore()
 
-    @pl.loop(1, devices)
-    def _(k):
-        pl.semaphore_signal(barrier, inc=1, device_id=place(k), device_id_type=MESH)
+    def greet(r, c):
+        pl.semaphore_signal(barrier, inc=1, device_id=(r, c), device_id_type=MESH)
+
+    peers(greet)
 
     sends = []
 
@@ -129,12 +142,6 @@
     _, b, c = partials_low(lambda i: ext[i], nx)
     sx[0], sx[1] = b, c
     sx[2] = partials_high(lambda i: ext[i])[2]
-    pl.semaphore_wait(barrier, devices - 1)
-    send(sx.at[pl.ds(0, 2)], ext.at[pl.ds(nx + 1, 2)], (up_r, col))
-    send(sx.at[2], ext.at[nx + 5], (dn_r, col))
-    send(ext.at[nx - 2], ext.at[nx], (up_r, col))
-    send(ext.at[0], ext.at[nx + 3], (dn_r, col))
-    send(ext.at[2], ext.at[nx + 4], (dn_r, col))
     loads[2].wait()
     for fetch in fetched:
         fetch.wait()
@@ -150,6 +157,12 @@
             for i in range(3):
                 sc[9 * d + 3 * i + k] = got[i]
 
+    pl.semaphore_wait(barrier, devices - 1)
+    send(sx.at[pl.ds(0, 2)], ext.at[pl.ds(nx + 1, 2)], (up_r, col))
+    send(sx.at[2], ext.at[nx + 5], (dn_r, col))
+    send(ext.at[nx - 2], ext.at[nx], (up_r, col))
+    send(ext.at[0], ext.at[nx + 3], (dn_r, col))
+    send(ext.at[2], ext.at[nx + 4], (dn_r, col))
     send(su.at[pl.ds(0, 3)], u.at[pl.ds(0, 3)], (row, up_c))
     send(su.at[pl.ds(3, 3)], u.at[pl.ds(3, 3)], (row, dn_c))
     for d in range(4):
@@ -242,25 +255,21 @@
     part[...] = line
     slots[me] = line
 
-    def spread(k):
-        t = lax.rem(me + k, devices)
-        return pltpu.make_async_remote_copy(
-            src_ref=part, dst_ref=slots.at[me], send_sem=g_send.at[t],
-            recv_sem=g_recv.at[me], device_id=place(k), device_id_type=MESH,
-        )
-
-    @pl.loop(1, devices)
-    def _(k):
-        spread(k).start()
-
-    @pl.loop(1, devices)
-    def _(k):
-        t = lax.rem(me + k, devices)
+    def spread(r, c):
+        pltpu.make_async_remote_copy(
+            src_ref=part, dst_ref=slots.at[me], send_sem=g_send.at[r * n_col + c],
+            recv_sem=g_recv.at[me], device_id=(r, c), device_id_type=MESH,
+        ).start()
+
+    def gather(r, c):
+        t = r * n_col + c
         pltpu.make_async_remote_copy(
             src_ref=part, dst_ref=slots.at[t], send_sem=g_send.at[t],
-            recv_sem=g_recv.at[t], device_id=place(k), device_id_type=MESH,
+            recv_sem=g_recv.at[t], device_id=(r, c), device_id_type=MESH,
         ).wait()
 
+    peers(spread)
+    peers(gather)
     for g in range(groups):
         at = pl.ds(g * grp, grp)
         pltpu.make_async_copy(out_ref.at[at], out_hbm.at[at], o_sem.at[g]).wait()

time: 33.4 us -> 33.5 us (level)
  no operation moved by 1% of the time
where the time goes in v3:
time: 33.5 us; the launch traced here: 33.3 us
  Pallas kernels  28.1 us (84%)
  local copies, waits for them, and re-layouts  4.53 us (14%)
  between operations  0.64 us (2%)
    pallas_call x1, Pallas kernels, shards(): pl.pallas_call(functools.partial(kernel, n_row, n_col, grp), out_shape=(j...  28.1 us
    unnamed x1, local copies, waits for them, and re-layouts  3.18 us
    pallas_call x1, local copies, waits for them, and re-layouts, shards(): pl.pallas_call(functools.partial(kernel, n_row, n_col, grp), out_shape=(j...  1.35 us

profile of v3, /device:TPU:0, one launch (start us, length us, event | category | flops | bytes accessed | tf_op | source)
XLA Modules:
  0.0 33.3 jit_solution(4955546275811725601)
XLA Ops:
  0.6 28.1 %shard_map.104 = (f32[32,32,512]{2,1,0:T(8,128)}, f32[16,4]{1,0:T(8,128)}) custom-call(s32[1,1,2]{2,1,0:T(1,128)} %cut_hbm.1, s32[1,1,2]{2,1,0:T(1,128)} %map_hbm.1, f32[32,32,512]{2,1,0:T(8,128)} %p_ref.1, bf16[48,256]{1,0:T(8,128)(2,1)} %constant.12.clone.refs_0_, bf16[256,256]{1,0:T(8,128)(2,1)} %constant.13.clone.refs_1_, ...), custom_call_target="tpu_custom_call" | custom-call | tf_op jit(solution)/shard_map/pallas_call | solution.py:313
  28.7 1.3 %copy.11 = f32[16,4]{0,1:T(4,128)} copy(f32[16,4]{1,0:T(8,128)} %get-tuple-element.3) | data formatting | bytes 512 | tf_op jit(solution)/shard_map/pallas_call | solution.py:313
  30.1 3.2 %copy.13 = f32[32,32,512]{2,1,0:T(8,128)} copy(f32[32,32,512]{2,1,0:T(8,128)} %get-tuple-element.6) | data formatting | bytes 4194304

commit v4 on v3

--- a/solution.py
+++ b/solution.py
@@ -251,7 +251,7 @@
     for z in range(zb):
         for n in range(n_lev):
             mass = jnp.sum(totals[n][:, z * width : (z + 1) * width], keepdims=True) / cells
-            line += jnp.where(lane == map_ref[0, 0, z] * n_lev + n, mass, 0.0)
+            line += jnp.where(lane == n * GROUPS + map_ref[0, 0, z], mass, 0.0)
     part[...] = line
     slots[me] = line
 
@@ -275,15 +275,27 @@
         pltpu.make_async_copy(out_ref.at[at], out_hbm.at[at], o_sem.at[g]).wait()
 
     total = jnp.sum(slots[...], axis=0)
-    wide = jnp.broadcast_to(total, (GROUPS, 128))
-    at_row = lax.broadcasted_iota(jnp.int32, (GROUPS, 128), 0)
-    at_lane = lax.broadcasted_iota(jnp.int32, (GROUPS, 128), 1)
-    at_col = lax.broadcasted_iota(jnp.int32, (GROUPS, n_lev), 1)
-    result = jnp.zeros((GROUPS, n_lev), F32)
-    for n in range(n_lev):
-        pick = jnp.where(at_lane == at_row * n_lev + n, wide, 0.0)
-        result = jnp.where(at_col == n, jnp.sum(pick, axis=1, keepdims=True), result)
-    mass_ref[...] = result
+    mass_ref[...] = jnp.concatenate(
+        [total[:, n * GROUPS : (n + 1) * GROUPS] for n in range(n_lev)], 0
+    )
+
+
+def deliver(c_hbm, m_hbm, out_hbm, mass_hbm, held, line, sems, m_sems):
+    count = sems.shape[1]
+    size = held.shape[0] // count
+    piece = [pl.ds(i * size, size) for i in range(count)]
+    copy = pltpu.make_async_copy
+    ins = [copy(c_hbm.at[p], held.at[p], sems.at[0, i]) for i, p in enumerate(piece)]
+    outs = [copy(held.at[p], out_hbm.at[p], sems.at[1, i]) for i, p in enumerate(piece)]
+    ins.insert(1, copy(m_hbm, line, m_sems.at[0]))
+    outs.insert(1, copy(line, mass_hbm, m_sems.at[1]))
+    for c in ins:
+        c.start()
+    for c, o in zip(ins, outs, strict=True):
+        c.wait()
+        o.start()
+    for o in outs:
+        o.wait()
 
 
 def solution(mesh):
@@ -310,11 +322,11 @@
         weights = [jnp.asarray(w, BF16) for w in (ws, wy, wu, wx, wc, cyclic_matrix(nz).T)]
         vmem = pl.BlockSpec(memory_space=pltpu.VMEM)
         hbm = pl.BlockSpec(memory_space=pl.ANY)
-        return pl.pallas_call(
+        found = pl.pallas_call(
             functools.partial(kernel, n_row, n_col, grp),
             out_shape=(
                 jax.ShapeDtypeStruct((nx, ny, nz), F32),
-                jax.ShapeDtypeStruct((GROUPS, len(LEVELS)), F32),
+                jax.ShapeDtypeStruct((len(LEVELS), GROUPS), F32),
             ),
             in_specs=[hbm] * 9,
             out_specs=(hbm, vmem),
@@ -344,6 +356,20 @@
                 collective_id=0, has_side_effects=True, vmem_limit_bytes=62 * 2**20
             ),
         )(cut_exponent, group_map, pressure, *weights)
+        coeffs, mass = pl.pallas_call(
+            deliver,
+            out_shape=tuple(jax.ShapeDtypeStruct(f.shape, F32) for f in found),
+            in_specs=[hbm] * 2,
+            out_specs=(hbm, hbm),
+            scratch_shapes=[
+                pltpu.VMEM((nx, ny, nz), F32),
+                pltpu.VMEM(found[1].shape, F32),
+                pltpu.SemaphoreType.DMA((2, 8)),
+                pltpu.SemaphoreType.DMA((2,)),
+            ],
+            compiler_params=pltpu.CompilerParams(vmem_limit_bytes=62 * 2**20),
+        )(*found)
+        return coeffs, mass.T
 
     specs = P("row", "col", None)
     return jax.shard_map(

time: 33.5 us -> 31.5 us (0.940)
  local copies, waits for them, and re-layouts: 4.53 us -> 0 us
  Pallas kernels: 28.1 us -> 30.7 us
    unnamed x1 -> x0, local copies, waits for them, and re-layouts: 3.18 us -> none
    pallas_call x0 -> x1, Pallas kernels: none -> 2.63 us  [shards(): pl.pallas_call(deliver, out_shape=tuple((jax.ShapeDtypeStruct(f.shape, F3...]
    pallas_call x1 -> x0, local copies, waits for them, and re-layouts: 1.35 us -> none  [shards(): pl.pallas_call(functools.partial(kernel, n_row, n_col, grp), out_shape=(j...]
where the time goes in v4:
time: 31.5 us; the launch traced here: 31.4 us
  Pallas kernels  30.7 us (97%)
  between operations  0.64 us (2%)
    pallas_call x1, Pallas kernels, shards(): pl.pallas_call(functools.partial(kernel, n_row, n_col, grp), out_shape=(j...  28.1 us
    pallas_call x1, Pallas kernels, shards(): pl.pallas_call(deliver, out_shape=tuple((jax.ShapeDtypeStruct(f.shape, F3...  2.63 us

profile of v4, /device:TPU:0, one launch (start us, length us, event | category | flops | bytes accessed | tf_op | source)
XLA Modules:
  0.0 31.4 jit_solution(1935948095838014302)
XLA Ops:
  0.6 28.1 %shard_map.104 = (f32[32,32,512]{2,1,0:T(8,128)}, f32[4,16]{1,0:T(4,128)}) custom-call(s32[1,1,2]{2,1,0:T(1,128)} %cut_hbm.1, s32[1,1,2]{2,1,0:T(1,128)} %map_hbm.1, f32[32,32,512]{2,1,0:T(8,128)} %p_ref.1, bf16[48,256]{1,0:T(8,128)(2,1)} %constant.12.clone.refs_0_, bf16[256,256]{1,0:T(8,128)(2,1)} %constant.13.clone.refs_1_, ...), custom_call_target="tpu_custom_call" | custom-call | tf_op jit(solution)/shard_map/pallas_call | solution.py:325
  28.7 2.6 %shard_map.105 = (f32[32,32,512]{2,1,0:T(8,128)}, f32[4,16]{1,0:T(4,128)}) custom-call(f32[32,32,512]{2,1,0:T(8,128)} %get-tuple-element.6.c_hbm, f32[4,16]{1,0:T(4,128)} %get-tuple-element.7.m_hbm), custom_call_target="tpu_custom_call" | custom-call | tf_op jit(solution)/shard_map/pallas_call | solution.py:359

commit v5 on v4

--- a/solution.py
+++ b/solution.py
@@ -78,7 +78,7 @@
     ext, q, sx, su, u, sc, cb, part, slots, out_ref, cut_ref, map_ref = refs[2:14]
     held = refs[14:20]
     ws_ref, wy_ref, wu_ref, wx_ref, wc_ref, wz_ref = held
-    in_sem, o_sem, w_sem, h_send, h_recv, g_send, g_recv = refs[20:]
+    in_sem, o_sem, w_sem, h_send, h_recv, g_send, g_recv, hop_sem = refs[20:]
     nx, ny, nz = p_ref.shape
     devices = n_row * n_col
     row, col = lax.axis_index("row"), lax.axis_index("col")
@@ -124,7 +124,21 @@
     def greet(r, c):
         pl.semaphore_signal(barrier, inc=1, device_id=(r, c), device_id_type=MESH)
 
-    peers(greet)
+    for r, c in ((up_r, col), (dn_r, col), (row, up_c), (row, dn_c)):
+        greet(r, c)
+    along_col = max(n_col // 2 - 1, 1)
+    hops = along_col + n_row // 2
+
+    def call(k):
+        aim = ((row, up_c), (row, dn_c)) if k < along_col else ((up_r, col), (dn_r, col))
+        for to in aim:
+            pl.semaphore_signal(hop_sem.at[k], inc=1, device_id=to, device_id_type=MESH)
+
+    def relay(k):
+        pl.semaphore_wait(hop_sem.at[k], 2)
+        if k + 1 < hops:
+            call(k + 1)
+
 
     sends = []
 
@@ -157,7 +171,8 @@
             for i in range(3):
                 sc[9 * d + 3 * i + k] = got[i]
 
-    pl.semaphore_wait(barrier, devices - 1)
+    pl.semaphore_wait(barrier, 4)
+    call(0)
     send(sx.at[pl.ds(0, 2)], ext.at[pl.ds(nx + 1, 2)], (up_r, col))
     send(sx.at[2], ext.at[nx + 5], (dn_r, col))
     send(ext.at[nx - 2], ext.at[nx], (up_r, col))
@@ -165,6 +180,7 @@
     send(ext.at[2], ext.at[nx + 4], (dn_r, col))
     send(su.at[pl.ds(0, 3)], u.at[pl.ds(0, 3)], (row, up_c))
     send(su.at[pl.ds(3, 3)], u.at[pl.ds(3, 3)], (row, dn_c))
+    relay(0)
     for d in range(4):
         to = (up_r if d < 2 else dn_r, up_c if d % 2 == 0 else dn_c)
         send(sc.at[pl.ds(9 * d, 9)], cb.at[pl.ds(9 * d, 9)], to)
@@ -172,13 +188,16 @@
     for g in range(nx // grp):
         at = pl.ds(g * grp, grp)
         q[at] = dot2(wy_ref[...], ext[at].reshape(grp * ny, nz)).reshape(grp, ny, nz)
+    relay(1)
     for copy in sends[5:7]:
         copy.wait_recv()
+    relay(2)
     for g in range(nx // grp):
         at = pl.ds(g * grp, grp)
         more = dot2(wu_ref[...], u[:, at, :].reshape(6 * grp, nz))
         q[at] += more.reshape(grp, ny, nz)
     half = nx // 2
+    relay(3)
 
     def x_lift(low, high):
         @pl.loop(0, ny // 8)
@@ -233,6 +252,8 @@
     totals = tuple(jnp.zeros((8, nz), F32) for _ in LEVELS)
     x_lift(grp // 2, half - grp // 2)
     totals = lax.fori_loop(1, groups - 1, z_group, totals)
+    for k in range(4, hops):
+        relay(k)
     for copy in sends[:5] + sends[7:]:
         copy.wait_recv()
     for copy in sends:
@@ -351,6 +372,7 @@
                 pltpu.SemaphoreType.DMA((11,)),
                 pltpu.SemaphoreType.DMA((devices,)),
                 pltpu.SemaphoreType.DMA((devices,)),
+                pltpu.SemaphoreType.REGULAR((n_col // 2 + n_row // 2,)),
             ],
             compiler_params=pltpu.CompilerParams(
                 collective_id=0, has_side_effects=True, vmem_limit_bytes=62 * 2**20

time: 31.5 us -> 29.3 us (0.930)
  Pallas kernels: 30.7 us -> 28.4 us
    pallas_call x1, Pallas kernels: 28.1 us -> 25.8 us  [shards(): pl.pallas_call(functools.partial(kernel, n_row, n_col, grp), out_shape=(j...]
where the time goes in v5:
time: 29.3 us; the launch traced here: 29.1 us
  Pallas kernels  28.4 us (97%)
  between operations  0.64 us (2%)
    pallas_call x1, Pallas kernels, shards(): pl.pallas_call(functools.partial(kernel, n_row, n_col, grp), out_shape=(j...  25.8 us
    pallas_call x1, Pallas kernels, shards(): pl.pallas_call(deliver, out_shape=tuple((jax.ShapeDtypeStruct(f.shape, F3...  2.63 us

profile of v5, /device:TPU:0, one launch (start us, length us, event | category | flops | bytes accessed | tf_op | source)
XLA Modules:
  0.0 29.1 jit_solution(6859429202715518759)
XLA Ops:
  0.6 25.8 %shard_map.104 = (f32[32,32,512]{2,1,0:T(8,128)}, f32[4,16]{1,0:T(4,128)}) custom-call(s32[1,1,2]{2,1,0:T(1,128)} %cut_hbm.1, s32[1,1,2]{2,1,0:T(1,128)} %map_hbm.1, f32[32,32,512]{2,1,0:T(8,128)} %p_ref.1, bf16[48,256]{1,0:T(8,128)(2,1)} %constant.12.clone.refs_0_, bf16[256,256]{1,0:T(8,128)(2,1)} %constant.13.clone.refs_1_, ...), custom_call_target="tpu_custom_call" | custom-call | tf_op jit(solution)/shard_map/pallas_call | solution.py:346
  26.4 2.6 %shard_map.105 = (f32[32,32,512]{2,1,0:T(8,128)}, f32[4,16]{1,0:T(4,128)}) custom-call(f32[32,32,512]{2,1,0:T(8,128)} %get-tuple-element.6.c_hbm, f32[4,16]{1,0:T(4,128)} %get-tuple-element.7.m_hbm), custom_call_target="tpu_custom_call" | custom-call | tf_op jit(solution)/shard_map/pallas_call | solution.py:381

commit v6 on v5

--- a/solution.py
+++ b/solution.py
@@ -175,21 +175,21 @@
     call(0)
     send(sx.at[pl.ds(0, 2)], ext.at[pl.ds(nx + 1, 2)], (up_r, col))
     send(sx.at[2], ext.at[nx + 5], (dn_r, col))
-    send(ext.at[nx - 2], ext.at[nx], (up_r, col))
     send(ext.at[0], ext.at[nx + 3], (dn_r, col))
-    send(ext.at[2], ext.at[nx + 4], (dn_r, col))
     send(su.at[pl.ds(0, 3)], u.at[pl.ds(0, 3)], (row, up_c))
     send(su.at[pl.ds(3, 3)], u.at[pl.ds(3, 3)], (row, dn_c))
     relay(0)
     for d in range(4):
         to = (up_r if d < 2 else dn_r, up_c if d % 2 == 0 else dn_c)
         send(sc.at[pl.ds(9 * d, 9)], cb.at[pl.ds(9 * d, 9)], to)
+    send(ext.at[nx - 2], ext.at[nx], (up_r, col))
+    send(ext.at[2], ext.at[nx + 4], (dn_r, col))
 
     for g in range(nx // grp):
         at = pl.ds(g * grp, grp)
         q[at] = dot2(wy_ref[...], ext[at].reshape(grp * ny, nz)).reshape(grp, ny, nz)
     relay(1)
-    for copy in sends[5:7]:
+    for copy in sends[3:5]:
         copy.wait_recv()
     relay(2)
     for g in range(nx // grp):
@@ -254,7 +254,7 @@
     totals = lax.fori_loop(1, groups - 1, z_group, totals)
     for k in range(4, hops):
         relay(k)
-    for copy in sends[:5] + sends[7:]:
+    for copy in sends[:3] + sends[5:]:
         copy.wait_recv()
     for copy in sends:
         copy.wait_send()

time: 29.3 us -> 30 us (1.024)
  Pallas kernels: 28.4 us -> 29.2 us
    pallas_call x1, Pallas kernels: 25.8 us -> 26.6 us  [shards(): pl.pallas_call(functools.partial(kernel, n_row, n_col, grp), out_shape=(j...]
where the time goes in v6:
time: 30 us; the launch traced here: 29.9 us
  Pallas kernels  29.2 us (97%)
  between operations  0.64 us (2%)
    pallas_call x1, Pallas kernels, shards(): pl.pallas_call(functools.partial(kernel, n_row, n_col, grp), out_shape=(j...  26.6 us
    pallas_call x1, Pallas kernels, shards(): pl.pallas_call(deliver, out_shape=tuple((jax.ShapeDtypeStruct(f.shape, F3...  2.63 us

profile of v6, /device:TPU:0, one launch (start us, length us, event | category | flops | bytes accessed | tf_op | source)
XLA Modules:
  0.0 29.9 jit_solution(9729548961149418612)
XLA Ops:
  0.6 26.6 %shard_map.104 = (f32[32,32,512]{2,1,0:T(8,128)}, f32[4,16]{1,0:T(4,128)}) custom-call(s32[1,1,2]{2,1,0:T(1,128)} %cut_hbm.1, s32[1,1,2]{2,1,0:T(1,128)} %map_hbm.1, f32[32,32,512]{2,1,0:T(8,128)} %p_ref.1, bf16[48,256]{1,0:T(8,128)(2,1)} %constant.12.clone.refs_0_, bf16[256,256]{1,0:T(8,128)(2,1)} %constant.13.clone.refs_1_, ...), custom_call_target="tpu_custom_call" | custom-call | tf_op jit(solution)/shard_map/pallas_call | solution.py:346
  27.2 2.6 %shard_map.105 = (f32[32,32,512]{2,1,0:T(8,128)}, f32[4,16]{1,0:T(4,128)}) custom-call(f32[32,32,512]{2,1,0:T(8,128)} %get-tuple-element.6.c_hbm, f32[4,16]{1,0:T(4,128)} %get-tuple-element.7.m_hbm), custom_call_target="tpu_custom_call" | custom-call | tf_op jit(solution)/shard_map/pallas_call | solution.py:381

commit v7 on v5

--- a/solution.py
+++ b/solution.py
@@ -86,6 +86,29 @@
     up_r, dn_r = lax.rem(row + 1, n_row), lax.rem(row + n_row - 1, n_row)
     up_c, dn_c = lax.rem(col + 1, n_col), lax.rem(col + n_col - 1, n_col)
 
+    def wrap(value, size):
+        return lax.select(value >= size, value - size, value)
+
+    def peers(visit):
+        @pl.loop(1, n_row)
+        def _(j):
+            other = wrap(row + j, n_row)
+
+            @pl.loop(0, n_col)
+            def _(k):
+                visit(other, wrap(col + k, n_col))
+
+        @pl.loop(1, n_col)
+        def _(k):
+            visit(row, wrap(col + k, n_col))
+
+    barrier = pltpu.get_barrier_semaphore()
+
+    def greet(r, c):
+        pl.semaphore_signal(barrier, inc=1, device_id=(r, c), device_id_type=MESH)
+
+    for r, c in ((up_r, col), (dn_r, col), (row, up_c), (row, dn_c)):
+        greet(r, c)
     pieces = ((0, 8), (nx - 8, 8), (8, nx - 16))
     loads = []
     for i, (at, size) in enumerate(pieces):
@@ -103,29 +126,6 @@
         fetch.start()
         fetched.append(fetch)
 
-    def wrap(value, size):
-        return lax.select(value >= size, value - size, value)
-
-    def peers(visit):
-        @pl.loop(1, n_col)
-        def _(k):
-            visit(row, wrap(col + k, n_col))
-
-        @pl.loop(1, n_row)
-        def _(j):
-            other = wrap(row + j, n_row)
-
-            @pl.loop(0, n_col)
-            def _(k):
-                visit(other, wrap(col + k, n_col))
-
-    barrier = pltpu.get_barrier_semaphore()
-
-    def greet(r, c):
-        pl.semaphore_signal(barrier, inc=1, device_id=(r, c), device_id_type=MESH)
-
-    for r, c in ((up_r, col), (dn_r, col), (row, up_c), (row, dn_c)):
-        greet(r, c)
     along_col = max(n_col // 2 - 1, 1)
     hops = along_col + n_row // 2
 

time: 29.3 us -> 29.2 us (level)
  no operation moved by 1% of the time
where the time goes in v7:
time: 29.2 us; the launch traced here: 29 us
  Pallas kernels  28.4 us (97%)
  between operations  0.64 us (2%)
    pallas_call x1, Pallas kernels, shards(): pl.pallas_call(functools.partial(kernel, n_row, n_col, grp), out_shape=(j...  25.7 us
    pallas_call x1, Pallas kernels, shards(): pl.pallas_call(deliver, out_shape=tuple((jax.ShapeDtypeStruct(f.shape, F3...  2.63 us

profile of v7, /device:TPU:0, one launch (start us, length us, event | category | flops | bytes accessed | tf_op | source)
XLA Modules:
  0.0 29.0 jit_solution(10507710857274675626)
XLA Ops:
  0.6 25.7 %shard_map.104 = (f32[32,32,512]{2,1,0:T(8,128)}, f32[4,16]{1,0:T(4,128)}) custom-call(s32[1,1,2]{2,1,0:T(1,128)} %cut_hbm.1, s32[1,1,2]{2,1,0:T(1,128)} %map_hbm.1, f32[32,32,512]{2,1,0:T(8,128)} %p_ref.1, bf16[48,256]{1,0:T(8,128)(2,1)} %constant.12.clone.refs_0_, bf16[256,256]{1,0:T(8,128)(2,1)} %constant.13.clone.refs_1_, ...), custom_call_target="tpu_custom_call" | custom-call | tf_op jit(solution)/shard_map/pallas_call | solution.py:346
  26.4 2.6 %shard_map.105 = (f32[32,32,512]{2,1,0:T(8,128)}, f32[4,16]{1,0:T(4,128)}) custom-call(f32[32,32,512]{2,1,0:T(8,128)} %get-tuple-element.6.c_hbm, f32[4,16]{1,0:T(4,128)} %get-tuple-element.7.m_hbm), custom_call_target="tpu_custom_call" | custom-call | tf_op jit(solution)/shard_map/pallas_call | solution.py:381
